TPU v7x, 32 devices: a whole 2x2x4 slice. The times are simulated.
32 devices in a mesh: groups: 2 (over y), row: 4 (over z), col: 2 (over x), sub: 2 (over core).
Axes of the slice: x: 2, y: 2, z: 4, core: 2. Of those that a mesh axis runs over, the one named last changes fastest.
Arguments:
- matrix: float32 [16384, 8192], P(('groups', 'row'), ('col', 'sub')), parts along dimension 0, may hold values from -60 to 60
- basis_vectors: float32 [16384, 1024], P(('groups', 'row'), ('col', 'sub')), parts along dimension 0, may hold values from -0.0625 to 0.0625
- split_size: int32 [2], P('groups'), parts along dimension 0, may hold values from 256 to 767
Outputs:
- children: float32 [2, 2048, 1024], P('sub', ('groups', 'row'), 'col'), parts along dimension 1
There are 2 independent parts, one for each index of `groups`. A program takes and returns all parts, laid end to end along the dimension named above; each array names one. Nothing has to cross between parts.
Inputs may be any that keep to these rules, and one draw needn't show every extreme that they name: The second subspace has 1024 minus split_size vectors.
All inputs are finite; a program needn't handle non-finite values.
Results may differ from a plain program's by a relative error of at most 0.00011.
Values sent between devices are 32-bit elements; how exact they have to be, the bound alone decides.
A program may use at most 128 MiB of HBM per device.

v0:
```python
import jax
import jax.numpy as jnp
from jax import lax
from jax.sharding import PartitionSpec as P


def shards(matrix, basis_vectors, split_size):
    strip = lax.all_gather(basis_vectors, "row", axis=0, tiled=True)
    row_panel = lax.all_to_all(strip, ("col", "sub"), split_axis=0, concat_axis=1, tiled=True)
    partial_image = jnp.dot(
        matrix, row_panel, precision=lax.Precision.HIGHEST, preferred_element_type=jnp.float32
    )
    image = lax.psum_scatter(partial_image, ("col", "sub"), scatter_dimension=1, tiled=True)
    partial_proj = lax.dot_general(
        lax.all_gather(basis_vectors, ("col", "sub"), axis=1, tiled=True),
        image,
        (((0,), (0,)), ((), ())),
        precision=lax.Precision.HIGHEST,
        preferred_element_type=jnp.float32,
    )
    proj_block = lax.psum_scatter(partial_proj, "row", scatter_dimension=0, tiled=True)
    child_block = lax.all_gather(proj_block, "sub", axis=1, tiled=True)
    row_ids = (
        jnp.arange(child_block.shape[0], dtype=jnp.int32)
        + lax.axis_index("row") * child_block.shape[0]
    )
    col_ids = (
        jnp.arange(child_block.shape[1], dtype=jnp.int32)
        + lax.axis_index("col") * child_block.shape[1]
    )
    leading = split_size[0]
    row_first = row_ids < leading
    col_first = col_ids < leading
    mask_one = row_first[:, None] & col_first[None, :]
    mask_two = jnp.logical_not(row_first)[:, None] & jnp.logical_not(col_first)[None, :]
    selected = jnp.where(lax.axis_index("sub") == 0, mask_one, mask_two)
    return jnp.where(selected, child_block, jnp.zeros((), jnp.float32))[None]


def solution(mesh):
    placed = (
        P(("groups", "row"), ("col", "sub")),
        P(("groups", "row"), ("col", "sub")),
        P("groups"),
    )
    return jax.shard_map(
        shards,
        mesh=mesh,
        in_specs=placed,
        out_specs=P("sub", ("groups", "row"), "col"),
        check_vma=False,
    )
```

profile of v0, /device:TPU:0, one launch (start us, length us, event | category | flops | bytes accessed | tf_op | source)
XLA Modules:
  0.0 493.2 jit_solution(18207130917740719552)
XLA Ops:
  6.5 0.0 all-gather.3.cloned.1.call-start
  6.5 0.7 all-gather.3.cloned.1.call-update
  7.3 0.0 all-gather.5.cloned.1.call-start
  7.3 0.7 all-gather.5.cloned.1.call-update
  8.0 0.0 reduce-scatter.3.cloned.1.call-start
  8.1 153.2 %all-gather.3.cloned.1.call-done = f32[8192,256]{1,0:T(8,128)} async-done(((f32[2048,256]{1,0:T(8,128)}), f32[8192,256]{1,0:T(8,128)}) %all-gather.3.cloned.1.call-update) | async-done | bytes 8388624 | tf_op jit(solution)/shard_map/all_gather | solution.py:8
  161.3 145.5 %all_to_all.19 = f32[4,2048,256]{2,1,0:T(8,128)} all-to-all(f32[4,2048,256]{2,1,0:T(8,128)} %bitcast.15), channel_id=1, replica_groups=mesh['groups'=2,'row'=4,'col'=2,'sub'=2] {'col','sub'}, dimensions={0} | all-to-all | bytes 16777216 | tf_op jit(solution)/shard_map/all_to_all | solution.py:9
  306.7 8.8 %copy.6 = f32[2048,4,256]{0,2,1:T(8,128)} copy(f32[2048,4,256]{2,0,1:T(8,128)} %bitcast.14) | data formatting | bytes 16777216 | tf_op jit(solution)/shard_map/all_to_all | solution.py:9
  315.5 60.4 %fusion.2 = f32[2048,1024]{1,0:T(8,128)} fusion(f32[2048,2048]{1,0:T(8,128)} %param.3, f32[2048,1024]{0,1:T(8,128)} %bitcast.16), kind=kOutput, calls=%fused_computation.6 | convolution fusion | flops 51539607552 | bytes 33554432 | tf_op jit(solution)/shard_map/dot_general | solution.py:10
  376.0 0.0 reduce-scatter.3.cloned.1.call-update
  376.0 0.2 reduce-scatter.5.cloned.1.call-start
  376.2 0.0 all-gather.5.cloned.1.call-done
  376.2 68.4 %reduce-scatter.3.cloned.1.call-done = f32[2048,256]{1,0:T(8,128)} async-done(((f32[2048,1024]{1,0:T(8,128)}), f32[2048,256]{1,0:T(8,128)}) %reduce-scatter.3.cloned.1.call-update) | async-done | bytes 2097168 | tf_op jit(solution)/shard_map/reduce_scatter | solution.py:13
  444.6 11.0 %convolution_bitcast_fusion = f32[1024,256]{0,1:T(8,128)} fusion(f32[2048,256]{1,0:T(8,128)} %reduce-scatter.3.cloned.1.call-done, f32[2048,1024]{1,0:T(8,128)} %all-gather.5.cloned.1.call-done), kind=kOutput, calls=%fused_computation | convolution fusion | flops 6442450944 | bytes 11534336 | tf_op jit(solution)/shard_map/dot_general | solution.py:14
  455.6 0.0 reduce-scatter.5.cloned.1.call-update
  456.3 26.8 %reduce-scatter.5.cloned.1.call-done = f32[256,256]{0,1:T(8,128)} async-done(((f32[1024,256]{0,1:T(8,128)}), f32[256,256]{0,1:T(8,128)}) %reduce-scatter.5.cloned.1.call-update) | async-done | bytes 262160 | tf_op jit(solution)/shard_map/reduce_scatter | solution.py:21
  483.1 2.4 all_gather.11
  485.5 0.2 select_bitcast_fusion
  485.7 1.0 copy.7
  (2 shorter events, 0.0 us)
Async XLA Ops:
  6.5 154.7 %all-gather.3.cloned.1.call-start = ((), (), s32[]{:S(2)}) async-start(), calls=%async_computation.3 | async-start | bytes 10485760 | tf_op jit(solution)/shard_map/all_gather | solution.py:8
  7.3 369.0 %all-gather.5.cloned.1.call-start = ((), (), s32[]{:S(2)}) async-start(), calls=%async_computation.5 | async-start | bytes 10485760 | tf_op jit(solution)/shard_map/all_gather | solution.py:15
  8.0 436.6 %reduce-scatter.3.cloned.1.call-start = ((), (), s32[]{:S(2)}) async-start(), calls=%async_computation.4 | async-start | bytes 10485760 | tf_op jit(solution)/shard_map/reduce_scatter | solution.py:13
  376.0 107.1 %reduce-scatter.5.cloned.1.call-start = ((), (), s32[]{:S(2)}) async-start(), calls=%async_computation.6 | async-start | bytes 1310720 | tf_op jit(solution)/shard_map/reduce_scatter | solution.py:21
Sparse Core Ops, SparseCore 0:
  8.9 152.3 all-gather.2
  162.8 101.4 all-gather.4
  376.1 68.5 reduce-scatter.2
  455.8 27.2 reduce-scatter.4
where the time goes:
time: 494 us; the launch traced here: 493 us
  waiting for transfers between devices  250 us (51%)
  blocking collectives  148 us (30%)
  matrix products  71.4 us (14%)
  between operations  13.8 us (3%)
  local copies, waits for them, and re-layouts  9.76 us (2%)
    all_gather x1, waiting for transfers between devices, shards(): strip = lax.all_gather(basis_vectors, 'row', axis=0, tiled=True)  153 us
    all_to_all x1, blocking collectives, shards(): lax.all_to_all(strip, ('col', 'sub'), split_axis=0, concat_axis=1, tiled=...  145 us
    reduce_scatter x1, waiting for transfers between devices, shards(): lax.psum_scatter(partial_image, ('col', 'sub'), scatter_dimension=1, tile...  68.4 us
    dot_general x1, matrix products, shards(): jnp.dot(matrix, row_panel, precision=lax.Precision.HIGHEST, preferred_ele...  60.4 us
    reduce_scatter x1, waiting for transfers between devices, shards(): lax.psum_scatter(partial_proj, 'row', scatter_dimension=0, tiled=True)  26.8 us
    dot_general x1, matrix products, shards(): lax.dot_general(lax.all_gather(basis_vectors, ('col', 'sub'), axis=1, til...  11 us
  transfers between devices with their start and end apart: 4, of which 3 were waited for; matrix products, arithmetic and copies ran while one was open for 14% of the time, Pallas kernels for 0%

commit v1 on v0

--- a/solution.py
+++ b/solution.py
@@ -5,7 +5,12 @@
 
 
 def shards(matrix, basis_vectors, split_size):
-    strip = lax.all_gather(basis_vectors, "row", axis=0, tiled=True)
+    ring = [basis_vectors]
+    for hop in range(3):
+        ring.append(lax.ppermute(ring[-1], "row", [(dev, (dev + 1) % 4) for dev in range(4)]))
+    strip = jnp.roll(
+        jnp.concatenate(ring[::-1], axis=0), (lax.axis_index("row") + 1) * ring[0].shape[0], axis=0
+    )
     row_panel = lax.all_to_all(strip, ("col", "sub"), split_axis=0, concat_axis=1, tiled=True)
     partial_image = jnp.dot(
         matrix, row_panel, precision=lax.Precision.HIGHEST, preferred_element_type=jnp.float32

time: 494 us -> 473 us (0.957)
  blocking collectives: 148 us -> 99.3 us
  local copies, waits for them, and re-layouts: 9.76 us -> 36.3 us
  waiting for transfers between devices: 250 us -> 240 us
  matrix products: 71.4 us -> 80 us
    all_gather x1 -> x0, waiting for transfers between devices: 153 us -> none  [shards(): strip = lax.all_gather(basis_vectors, 'row', axis=0, tiled=True)]
    ppermute x0 -> x3, waiting for transfers between devices: none -> 145 us  [shards(): lax.ppermute(ring[-1], 'row', [(dev, (dev + 1) % 4) for dev in range(4)])]
    all_to_all x1, blocking collectives: 145 us -> 96.9 us  [shards(): lax.all_to_all(strip, ('col', 'sub'), split_axis=0, concat_axis=1, tiled=...]
    unnamed x0 -> x13, local copies, waits for them, and re-layouts: none -> 21.2 us
    dot_general x1, matrix products: 60.4 us -> 68.8 us  [shards(): jnp.dot(matrix, row_panel, precision=lax.Precision.HIGHEST, preferred_ele...]
  transfers between devices with their start and end apart: 4 -> 6, of which waited for: 3 -> 5; matrix products, arithmetic and copies ran while one was open for 14% -> 22% of each run, Pallas kernels for 0% -> 0%
where the time goes in v1:
time: 473 us
  waiting for transfers between devices  240 us (51%)
  blocking collectives  99.3 us (21%)
  matrix products  80 us (17%)
  local copies, waits for them, and re-layouts  36.3 us (8%)
  between operations  13.8 us (3%)
    ppermute x3, waiting for transfers between devices, shards(): lax.ppermute(ring[-1], 'row', [(dev, (dev + 1) % 4) for dev in range(4)])  145 us
    all_to_all x1, blocking collectives, shards(): lax.all_to_all(strip, ('col', 'sub'), split_axis=0, concat_axis=1, tiled=...  96.9 us
    dot_general x1, matrix products, shards(): jnp.dot(matrix, row_panel, precision=lax.Precision.HIGHEST, preferred_ele...  68.8 us
    reduce_scatter x1, waiting for transfers between devices, shards(): lax.psum_scatter(partial_image, ('col', 'sub'), scatter_dimension=1, tile...  68.5 us
    reduce_scatter x1, waiting for transfers between devices, shards(): lax.psum_scatter(partial_proj, 'row', scatter_dimension=0, tiled=True)  26.8 us
    unnamed x13, local copies, waits for them, and re-layouts  21.2 us
    dot_general x1, matrix products, shards(): lax.dot_general(lax.all_gather(basis_vectors, ('col', 'sub'), axis=1, til...  11.1 us
  transfers between devices with their start and end apart: 6, of which 5 were waited for; matrix products, arithmetic and copies ran while one was open for 22% of the time, Pallas kernels for 0%

profile of v1, /device:TPU:0, one launch (start us, length us, event | category | flops | bytes accessed | tf_op | source)
XLA Modules:
  0.0 472.6 jit_solution(14732076714837908464)
XLA Ops:
  6.5 3.1 collective-permute-start
  9.6 47.9 %collective-permute-done = f32[2048,256]{1,0:T(8,128)S(1)} collective-permute-done((f32[2048,256]{1,0:T(8,128)}, f32[2048,256]{1,0:T(8,128)S(1)}, u32[]{:S(2)}, u32[]{:S(2)}) %collective-permute-start) | collective-permute-done | bytes 2097184 | tf_op jit(solution)/shard_map/ppermute | solution.py:10
  57.5 1.4 copy-done.1
  58.9 48.7 %collective-permute-done.1 = f32[2048,256]{1,0:T(8,128)} collective-permute-done((f32[2048,256]{1,0:T(8,128)S(1)}, f32[2048,256]{1,0:T(8,128)}, u32[]{:S(2)}, u32[]{:S(2)}) %collective-permute-start.1) | collective-permute-done | bytes 2097184 | tf_op jit(solution)/shard_map/ppermute | solution.py:10
  107.6 0.0 reduce-scatter.3.cloned.1.call-start
  107.7 47.9 %collective-permute-done.2 = f32[2048,256]{1,0:T(8,128)} collective-permute-done((f32[2048,256]{1,0:T(8,128)}, f32[2048,256]{1,0:T(8,128)}, u32[]{:S(2)}, u32[]{:S(2)}) %collective-permute-start.2) | collective-permute-done | bytes 2097184 | tf_op jit(solution)/shard_map/ppermute | solution.py:10
  155.6 3.1 constant_dynamic-update-slice_fusion.7
  158.7 3.0 constant_dynamic-update-slice_fusion.6
  161.7 3.0 constant_dynamic-update-slice_fusion.5
  164.8 3.1 constant_dynamic-update-slice_fusion.4
  167.9 3.1 constant_dynamic-update-slice_fusion.3
  171.0 3.0 constant_dynamic-update-slice_fusion.2
  174.0 1.5 constant_dynamic-update-slice_fusion.1
  175.5 1.4 constant_dynamic-update-slice_fusion
  176.9 3.9 constant_dynamic-slice_fusion
  180.8 96.9 %all_to_all.19 = f32[4,2048,256]{2,1,0:T(8,128)} all-to-all(f32[4,2048,256]{2,1,0:T(8,128)S(1)} %bitcast.16), channel_id=1, replica_groups=mesh['groups'=2,'row'=4,'col'=2,'sub'=2] {'col','sub'}, dimensions={0} | all-to-all | bytes 16777216 | tf_op jit(solution)/shard_map/all_to_all | solution.py:14
  277.7 8.8 %copy.6 = f32[2048,4,256]{0,2,1:T(8,128)} copy(f32[2048,4,256]{2,0,1:T(8,128)} %bitcast.17) | data formatting | bytes 16777216 | tf_op jit(solution)/shard_map/all_to_all | solution.py:14
  286.5 68.8 %convolution_bitcast_fusion = f32[2048,1024]{0,1:T(8,128)} fusion(f32[2048,1024]{0,1:T(8,128)} %bitcast.18, f32[2048,2048]{1,0:T(8,128)} %param.3), kind=kOutput, calls=%fused_computation | convolution fusion | flops 51539607552 | bytes 33554432 | tf_op jit(solution)/shard_map/dot_general | solution.py:15
  355.4 68.5 %reduce-scatter.3.cloned.1.call-done = f32[2048,256]{0,1:T(8,128)} async-done(((f32[2048,1024]{0,1:T(8,128)}), f32[2048,256]{0,1:T(8,128)}) %reduce-scatter.3.cloned.1.call-update) | async-done | bytes 2097168 | tf_op jit(solution)/shard_map/reduce_scatter | solution.py:18
  423.9 11.1 %convolution_bitcast_fusion.1 = f32[1024,256]{0,1:T(8,128)} fusion(f32[2048,256]{0,1:T(8,128)} %reduce-scatter.3.cloned.1.call-done, f32[2048,1024]{1,0:T(8,128)} %all-gather.2.cloned.1.call-done), kind=kOutput, calls=%fused_computation.1 | convolution fusion | flops 6442450944 | bytes 11534336 | tf_op jit(solution)/shard_map/dot_general | solution.py:19
  435.7 26.8 %reduce-scatter.5.cloned.1.call-done = f32[256,256]{0,1:T(8,128)} async-done(((f32[1024,256]{0,1:T(8,128)}), f32[256,256]{0,1:T(8,128)}) %reduce-scatter.5.cloned.1.call-update) | async-done | bytes 262160 | tf_op jit(solution)/shard_map/reduce_scatter | solution.py:26
  462.5 2.4 all_gather.7
  464.9 0.2 select_bitcast_fusion
  465.1 1.0 copy.7
  (15 shorter events, 0.1 us)
Async XLA Ops:
  6.5 168.9 %copy-start = (f32[2048,256]{1,0:T(8,128)S(1)}, f32[2048,256]{1,0:T(8,128)}, u32[]{:S(2)}) copy-start(f32[2048,256]{1,0:T(8,128)} %param.4) | copy-start | bytes 6291460
  6.5 348.9 %all-gather.2.cloned.1.call-start = ((), (), s32[]{:S(2)}) async-start(), calls=%async_computation.4 | async-start | bytes 10485760 | tf_op jit(solution)/shard_map/all_gather | solution.py:20
  6.5 51.0 %collective-permute-start = (f32[2048,256]{1,0:T(8,128)}, f32[2048,256]{1,0:T(8,128)S(1)}, u32[]{:S(2)}, u32[]{:S(2)}) collective-permute-start(f32[2048,256]{1,0:T(8,128)} %param.4), channel_id=1, source_target_pairs={{0,4},{4,8},{8,12},{12,0},{1,5},{5,9},{9,13},{13,1},{2,6},{6,10},{... | collective-permute-start | bytes 6291464 | tf_op jit(solution)/shard_map/ppermute | solution.py:10
  57.5 1.4 copy-start.1
  58.9 48.7 %collective-permute-start.1 = (f32[2048,256]{1,0:T(8,128)S(1)}, f32[2048,256]{1,0:T(8,128)}, u32[]{:S(2)}, u32[]{:S(2)}) collective-permute-start(f32[2048,256]{1,0:T(8,128)S(1)} %collective-permute-done), channel_id=1, source_target_pairs={{0,4},{4,8},{8,12},{12,0},{1,5},{5,9},{9,13},{13,1},{2,6},{6,10},{... | collective-permute-start | bytes 6291464 | tf_op jit(solution)/shard_map/ppermute | solution.py:10
  107.6 48.1 %collective-permute-start.2 = (f32[2048,256]{1,0:T(8,128)}, f32[2048,256]{1,0:T(8,128)}, u32[]{:S(2)}, u32[]{:S(2)}) collective-permute-start(f32[2048,256]{1,0:T(8,128)} %collective-permute-done.1), channel_id=1, source_target_pairs={{0,4},{4,8},{8,12},{12,0},{1,5},{5,9},{9,13},{13,1},{2,6},{6,10},{... | collective-permute-start | bytes 6291464 | tf_op jit(solution)/shard_map/ppermute | solution.py:10
  107.6 316.3 %reduce-scatter.3.cloned.1.call-start = ((), (), s32[]{:S(2)}) async-start(), calls=%async_computation.3 | async-start | bytes 10485760 | tf_op jit(solution)/shard_map/reduce_scatter | solution.py:18
  107.7 66.3 %copy-start.2 = (f32[2048,256]{1,0:T(8,128)S(1)}, f32[2048,256]{1,0:T(8,128)}, u32[]{:S(2)}) copy-start(f32[2048,256]{1,0:T(8,128)} %copy-done.1) | copy-start | bytes 6291460
  355.3 107.1 %reduce-scatter.5.cloned.1.call-start = ((), (), s32[]{:S(2)}) async-start(), calls=%async_computation.5 | async-start | bytes 1310720 | tf_op jit(solution)/shard_map/reduce_scatter | solution.py:26
Sparse Core Ops, SparseCore 0:
  107.7 59.5 all-gather.1
  355.5 68.3 reduce-scatter.2
  435.1 27.2 reduce-scatter.4
